TPU v7x, 512 devices: a whole 4x8x8 slice. The times are simulated.
512 devices in a mesh: cable: 256 (over z, y, x), win: 2 (over core).
Axes of the slice: x: 4, y: 8, z: 8, core: 2. Of those that a mesh axis runs over, the one named last changes fastest.
Arguments:
- records: bfloat16 [512, 8192, 128], P(None, 'cable', 'win'), may hold values from -60 to 60
Outputs:
- xcorr: float32 [8192, 64, 512], P('cable', None, 'win')
All inputs are finite; a program needn't handle non-finite values.
Results may differ from a plain program's by a relative error of at most 0.0064.
Values may be sent and summed in bfloat16 or wider, within the bound.
A program may use at most 128 MiB of HBM per device.

v0:
```python
import math

import jax
import jax.numpy as jnp
from jax import lax
from jax.sharding import PartitionSpec as P

OFFS = 64


epsilon = 1e-06


def total_of_pieces(array, axis):
    tiles = lax.all_gather(array, axis)
    return tiles.sum(axis=0)


def from_behind(block, axis, distance):
    devices = range(lax.axis_size(axis))
    route = [(i - distance, i) for i in devices if i - distance in devices]
    return lax.ppermute(block, axis, route)


def cut_along(array, dim, devices):
    dims = array.shape
    tiles = array.reshape(*dims[:dim], devices, dims[dim] // devices, *dims[dim + 1 :])
    return jnp.moveaxis(tiles, dim, 0)


def sent_and_summed(array, axis, dim):
    devices = lax.axis_size(axis)
    tiles = lax.all_to_all(cut_along(array, dim, devices), axis, 0, 0, tiled=True)
    return jnp.sum(tiles, axis=0)


def forward_table(samples):
    frequencies = samples // 2 + 1
    times = jnp.arange(samples, dtype=jnp.int32)[None, :]
    freq = jnp.arange(frequencies, dtype=jnp.int32)[:, None]
    phase = 2.0 * math.pi / samples * (freq * times % samples).astype(jnp.float32)
    taper = 0.5 - 0.5 * jnp.cos(2.0 * math.pi / samples * times.astype(jnp.float32))
    return jnp.concatenate([taper * jnp.cos(phase), -taper * jnp.sin(phase)], axis=0).astype(
        jnp.bfloat16
    )


def inverse_table(samples, lag_count, factor):
    frequencies = samples // 2 + 1
    freq = jnp.arange(frequencies, dtype=jnp.int32)[:, None]
    lagpos = jnp.arange(lag_count, dtype=jnp.int32)[None, :]
    phase = 2.0 * math.pi / samples * (freq * lagpos % samples).astype(jnp.float32)
    weight = jnp.where((freq == 0) | (freq == samples // 2), 1.0, 2.0).astype(jnp.float32) * factor
    return jnp.concatenate([weight * jnp.cos(phase), -weight * jnp.sin(phase)], axis=0)


def transform_back(cross_spec, inverse, channels, lag_count):
    result = lax.dot_general(
        cross_spec,
        inverse,
        (((0,), (0,)), ((), ())),
        precision=lax.Precision.HIGHEST,
        preferred_element_type=jnp.float32,
    )
    return result.reshape(channels, OFFS, lag_count)


def body(records):
    samples, channels, windows = records.shape
    frequencies = samples // 2 + 1
    total_windows = windows * lax.axis_size("win")
    table = forward_table(samples)
    spectra = jnp.dot(
        table, records.reshape(samples, channels * windows), preferred_element_type=jnp.float32
    )
    spectra = spectra.reshape(2 * frequencies, channels, windows)
    real_part = spectra[:frequencies]
    imag_part = spectra[frequencies:]
    power_sum = total_of_pieces(
        jnp.sum(real_part * real_part + imag_part * imag_part, axis=2), "win"
    )
    scaling = lax.rsqrt(power_sum / total_windows + epsilon)[:, :, None]
    packed = jnp.concatenate([real_part * scaling, imag_part * scaling], axis=2).astype(
        jnp.bfloat16
    )
    blocks_needed = (OFFS + channels - 1) // channels
    blocks = [packed]
    current = packed
    for neighbour in range(blocks_needed):
        current = from_behind(current, "cable", -1)
        blocks.append(current)
    partner = jnp.concatenate(blocks, axis=1)
    breadth = partner.shape[1]
    flipped = jnp.concatenate([packed[:, :, windows:], -packed[:, :, :windows]], axis=2)
    lefthand = jnp.concatenate([packed, flipped], axis=1)
    products = jnp.einsum("fxk,fmk->fxm", lefthand, partner, preferred_element_type=jnp.float32)
    products = products.reshape(frequencies, 2, channels * breadth)
    products = jnp.pad(products, ((0, 0), (0, 0), (0, channels + 1)))
    banded = products[:, :, 1 : 1 + channels * (breadth + 1)].reshape(
        frequencies, 2, channels, breadth + 1
    )
    banded = banded[:, :, :, :OFFS]
    cross_spec = jnp.transpose(banded, (1, 0, 2, 3)).reshape(2 * frequencies, channels * OFFS)
    factor = 1.0 / math.sqrt(2.0 * total_windows * frequencies)
    inverse = inverse_table(samples, samples, factor)
    terms = transform_back(cross_spec, inverse, channels, samples)
    return sent_and_summed(terms, "win", 2)


def solution(mesh):
    return jax.shard_map(
        body,
        mesh=mesh,
        in_specs=(P(None, "cable", "win"),),
        out_specs=P("cable", None, "win"),
        check_vma=False,
    )
```

profile of v0, /device:TPU:255, one launch (start us, length us, event | category | flops | bytes accessed | tf_op | source)
XLA Modules:
  0.0 242.2 jit_solution(17888233625217687463)
XLA Ops:
  0.0 0.0 copy-start
  0.1 2.3 multiply_convert_fusion.2
  2.4 0.0 copy-done
  2.4 1.3 fusion.23
  3.7 2.3 fusion.35
  6.1 2.2 copy.16
  8.3 3.5 %copy.17 = f32[257,2048]{0,1:T(8,128)} copy(f32[257,2048]{1,0:T(8,128)} %get-tuple-element.8) | data formatting | bytes 4210688 | tf_op jit(solution)/shard_map/slice | solution.py:78
  11.7 2.7 %add_reduce_fusion = f32[257,32]{0,1:T(8,128)S(1)} fusion(f32[257,2048]{0,1:T(8,128)} %copy.17, f32[257,2048]{0,1:T(8,128)S(1)} %copy.16), kind=kLoop, calls=%fused_computation.19 | loop fusion | flops 2097120 | bytes 4243584 | tf_op jit(solution)/shard_map/reduce_sum | solution.py:80
  14.4 2.2 all-gather.1
  16.7 0.1 copy.18
  16.8 5.3 %copy.19 = f32[257,32,64]{2,1,0:T(8,128)} copy(f32[257,32,64]{0,2,1:T(8,128)S(1)} %bitcast.30) | data formatting | bytes 4210688 | tf_op jit(solution)/shard_map/slice | solution.py:77
  22.1 6.8 %copy.20 = f32[257,32,64]{2,1,0:T(8,128)} copy(f32[257,32,64]{0,2,1:T(8,128)} %bitcast.31) | data formatting | bytes 4210688 | tf_op jit(solution)/shard_map/slice | solution.py:78
  28.9 0.0 copy-start.2
  28.9 4.1 %fusion.34 = (bf16[257,32,64]{2,1,0:T(8,128)(2,1)}, bf16[257,32,64]{2,1,0:T(8,128)(2,1)S(1)}) fusion(f32[257,32,64]{2,1,0:T(8,128)} %copy.19, f32[257,32]{1,0:T(8,128)S(1)} %copy.18), kind=kLoop, calls=%fused_computation.54 | loop fusion | flops 1579008 | bytes 4243584 | tf_op jit(solution)/shard_map/neg | solution.py:94
  33.0 0.0 copy-done.2
  33.0 1.7 multiply_convert_fusion
  34.7 0.0 copy-start.3
  34.7 1.3 copy-done.3
  36.0 1.2 pad_maximum_fusion
  37.2 2.5 %collective-permute-start = (bf16[257,32,128]{2,1,0:T(8,128)(2,1)S(1)}, bf16[257,32,128]{2,1,0:T(8,128)(2,1)}, u32[]{:S(2)}, u32[]{:S(2)}) collective-permute-start(bf16[257,32,128]{2,1,0:T(8,128)(2,1)S(1)} %pad_maximum_fusion), channel_id=1, source_target_pairs={{2,0},{4,2},{6,4},{8,6},{10,8},{12,10},{14,12},{16,14},{18,16},{20... | collective-permute-start | bytes 6316040 | tf_op jit(solution)/shard_map/ppermute | solution.py:22
  39.7 52.0 %collective-permute-done = bf16[257,32,128]{2,1,0:T(8,128)(2,1)} collective-permute-done((bf16[257,32,128]{2,1,0:T(8,128)(2,1)S(1)}, bf16[257,32,128]{2,1,0:T(8,128)(2,1)}, u32[]{:S(2)}, u32[]{:S(2)}) %collective-permute-start) | collective-permute-done | bytes 2105376 | tf_op jit(solution)/shard_map/ppermute | solution.py:22
  91.6 2.1 collective-permute-start.1
  93.7 2.2 broadcast_multiply_fusion
  95.9 1.1 maximum_bitcast_fusion
  97.0 1.9 dot_general.22
  99.0 46.4 %collective-permute-done.1 = bf16[257,32,128]{2,1,0:T(8,128)(2,1)} collective-permute-done((bf16[257,32,128]{2,1,0:T(8,128)(2,1)}, bf16[257,32,128]{2,1,0:T(8,128)(2,1)}, u32[]{:S(2)}, u32[]{:S(2)}) %collective-permute-start.1) | collective-permute-done | bytes 2105376 | tf_op jit(solution)/shard_map/ppermute | solution.py:22
  145.4 11.9 %fusion = f32[257,64,96]{2,1,0:T(8,128)} fusion(bf16[257,32,128]{2,1,0:T(8,128)(2,1)} %collective-permute-done.1, bf16[257,32,128]{2,1,0:T(8,128)(2,1)} %collective-permute-done, bf16[257,32,64]{2,1,0:T(8,128)(2,1)} %copy-done.3, bf16[257,32,64]{2,1,0:T(8,128)(2,1)S(1)} %get-tuple-element.6, bf16[257,32,64]{2,1,0:T(8,128)(2,1)} %get-tuple-element.5), kind=kOutput, calls=%fused_computation.1 | convolution fusion | flops 446332928 | bytes 13684736 | tf_op jit(solution)/shard_map/fxk,fmk->fxm/dot_general | solution.py:96
  157.3 11.8 %reshape.57 = f32[257,2,3072]{2,1,0:T(2,128)} reshape(f32[257,64,96]{2,1,0:T(8,128)} %fusion) | data formatting | bytes 12632064 | tf_op jit(solution)/shard_map/reshape | solution.py:97
  169.0 12.1 %pad_slice_fusion = f32[257,2,3104]{2,1,0:T(2,128)} fusion(f32[257,2,3072]{2,1,0:T(2,128)} %reshape.57), kind=kLoop, calls=%fused_computation | loop fusion | bytes 12697856 | tf_op jit(solution)/shard_map/slice | solution.py:99
  181.1 17.3 %copy.21 = f32[257,2,3104]{0,1,2:T(2,128)} copy(f32[257,2,3104]{2,1,0:T(2,128)} %pad_slice_fusion) | data formatting | bytes 12763648 | tf_op jit(solution)/shard_map/slice | solution.py:99
  198.4 9.0 %slice_bitcast_fusion = f32[2,257,32,64]{1,0,3,2:T(2,128)} fusion(f32[257,2,32,97]{0,1,3,2:T(2,128)} %bitcast.32), kind=kLoop, calls=%fused_computation.9 | loop fusion | bytes 8421376 | tf_op jit(solution)/shard_map/transpose | solution.py:103
  207.4 8.1 %reshape.59 = f32[514,2048]{0,1:T(8,128)} reshape(f32[2,257,32,64]{1,0,3,2:T(2,128)} %slice_bitcast_fusion) | data formatting | bytes 8421376 | tf_op jit(solution)/shard_map/reshape | solution.py:103
  215.5 12.1 %convolution_bitcast_fusion = f32[2,32,64,256]{3,2,0,1:T(8,128)S(1)} fusion(f32[32,64,514,1]{2,1,3,0:T(8,128)} %bitcast.33, f32[2,256,514]{1,0,2:T(2,128)S(1)} %dot_general.22), kind=kOutput, calls=%fused_computation.20 | convolution fusion | flops 6467616768 | bytes 9457664 | tf_op jit(solution)/shard_map/dot_general | solution.py:58
  227.6 0.5 copy.23
  228.1 0.0 copy-start.1
  228.1 10.0 %all_to_all.5 = f32[2,32,64,256]{3,2,1,0:T(8,128)} all-to-all(f32[2,32,64,256]{3,2,1,0:T(8,128)S(1)} %copy.23), channel_id=1, replica_groups=mesh['cable'=256,'win'=2] {'win'}, dimensions={0} | all-to-all | bytes 8388608 | tf_op jit(solution)/shard_map/all_to_all | solution.py:33
  238.1 4.1 %reduce_sum.29 = f32[32,64,256]{2,1,0:T(8,128)} reduce(f32[2,32,64,256]{3,2,1,0:T(8,128)} %all_to_all.5, f32[]{:T(128)} %constant.34.clone.1), dimensions={0}, to_apply=%region_2.3 | reduce | flops 524288 | bytes 6291460 | tf_op jit(solution)/shard_map/reduce_sum | solution.py:34
  242.2 0.0 copy-done.1
  (6 shorter events, 0.1 us)
Async XLA Ops:
  0.0 2.4 copy-start
  28.9 4.1 %copy-start.2 = (f32[257,32,64]{2,1,0:T(8,128)S(1)}, f32[257,32,64]{2,1,0:T(8,128)}, u32[]{:S(2)}) copy-start(f32[257,32,64]{2,1,0:T(8,128)} %copy.20) | copy-start | bytes 6316036
  34.7 1.3 copy-start.3
  37.2 54.4 %collective-permute-start = (bf16[257,32,128]{2,1,0:T(8,128)(2,1)S(1)}, bf16[257,32,128]{2,1,0:T(8,128)(2,1)}, u32[]{:S(2)}, u32[]{:S(2)}) collective-permute-start(bf16[257,32,128]{2,1,0:T(8,128)(2,1)S(1)} %pad_maximum_fusion), channel_id=1, source_target_pairs={{2,0},{4,2},{6,4},{8,6},{10,8},{12,10},{14,12},{16,14},{18,16},{20... | collective-permute-start | bytes 6316040 | tf_op jit(solution)/shard_map/ppermute | solution.py:22
  91.6 53.8 %collective-permute-start.1 = (bf16[257,32,128]{2,1,0:T(8,128)(2,1)}, bf16[257,32,128]{2,1,0:T(8,128)(2,1)}, u32[]{:S(2)}, u32[]{:S(2)}) collective-permute-start(bf16[257,32,128]{2,1,0:T(8,128)(2,1)} %collective-permute-done), channel_id=1, source_target_pairs={{2,0},{4,2},{6,4},{8,6},{10,8},{12,10},{14,12},{16,14},{18,16},{20... | collective-permute-start | bytes 6316040 | tf_op jit(solution)/shard_map/ppermute | solution.py:22
  228.1 14.1 %copy-start.1 = (bf16[512,32,64]{0,2,1:T(8,128)(2,1)S(1)}, bf16[512,32,64]{0,2,1:T(8,128)(2,1)}, u32[]{:S(2)}) copy-start(bf16[512,32,64]{0,2,1:T(8,128)(2,1)} %param.1) | copy-start | bytes 6291460
where the time goes:
time: 243 us; the launch traced here: 242 us
  waiting for transfers between devices  98.4 us (40%)
  local copies, waits for them, and re-layouts  82.2 us (34%)
  matrix products  25.2 us (10%)
  other arithmetic  19.4 us (8%)
  blocking collectives  12.2 us (5%)
  starting transfers between devices  4.55 us (2%)
    ppermute x2, waiting for transfers between devices, from_behind(): return lax.ppermute(block, axis, route)  98.4 us
    slice x2, local copies, waits for them, and re-layouts, body(): products[:, :, 1:1 + channels * (breadth + 1)]  29.4 us
    dot_general x1, matrix products, transform_back(): lax.dot_general(cross_spec, inverse, (((0,), (0,)), ((), ())), precision=...  12.1 us
    dot_general x1, matrix products, body(): jnp.einsum('fxk,fmk->fxm', lefthand, partner, preferred_element_type=jnp....  11.9 us
    reshape x1, local copies, waits for them, and re-layouts, body(): products = products.reshape(frequencies, 2, channels * breadth)  11.8 us
    slice x2, local copies, waits for them, and re-layouts, body(): imag_part = spectra[frequencies:]  10.3 us
    all_to_all x1, blocking collectives, sent_and_summed(): lax.all_to_all(cut_along(array, dim, devices), axis, 0, 0, tiled=True)  9.99 us
    slice x3, local copies, waits for them, and re-layouts, body(): real_part = spectra[:frequencies]  9.89 us
  transfers between devices with their start and end apart: 2, of which 2 were waited for; matrix products, arithmetic and copies ran while one was open for 2% of the time, Pallas kernels for 0%

commit v1 on v0

v1 whole, which is shorter than its diff:
```python
import functools
import math

import jax
import jax.numpy as jnp
import numpy as np
from jax import lax
from jax.experimental import pallas as pl
from jax.experimental.pallas import tpu as pltpu
from jax.sharding import PartitionSpec as P

MESH = pl.DeviceIdType.MESH

OFFS = 64
SAMPLES = 512
CH = 32
ROW = 4
SLOTS = 33
FREQS = ROW * SLOTS
PADDED = 136
LAGS = 256

epsilon = 1e-06


def slot_frequencies(parity):
    place = np.arange(PADDED)
    chip, slot = place // SLOTS, place % SLOTS
    half = np.where(slot < 32, 32 * chip + slot, 128)
    held = np.where(slot < 32, chip < ROW, (chip == ROW - 1) & (parity == 0))
    return (2 * half + parity)[:, None], held[:, None]


def angles(freq, times):
    return np.float32(2.0 * math.pi / SAMPLES) * (freq * times % SAMPLES).astype(np.float32)


def forward_table(parity):
    freq, held = slot_frequencies(parity)
    times = np.arange(SAMPLES)[None, :]
    phase = angles(freq, times)
    taper = np.float32(0.5) - np.float32(0.5) * np.cos(angles(1, times))
    taper = np.where(held, taper, np.float32(0.0))
    both = np.concatenate([taper * np.cos(phase), -taper * np.sin(phase)], axis=0)
    return both.astype(jnp.bfloat16)


def inverse_table(parity, factor):
    freq, held = slot_frequencies(parity)
    freq, held = freq[:FREQS], held[:FREQS]
    phase = angles(freq, np.arange(LAGS)[None, :])
    weight = np.where((freq == 0) | (freq == SAMPLES // 2), 1.0, 2.0) * held * factor
    weight = weight.astype(np.float32)
    both = np.stack([weight * np.cos(phase), -weight * np.sin(phase)], axis=1)
    return both.reshape(2 * FREQS, LAGS).astype(jnp.bfloat16)


def whiten_kernel(windows, table_ref, own_ref, other_ref, white_ref, re_buf, im_buf):
    core = lax.axis_index("win")

    @pl.loop(0, CH // 2, unroll=2)
    def _(pair):
        c = 2 * pair
        rhs = jnp.concatenate(
            [own_ref[c], other_ref[c], own_ref[c + 1], other_ref[c + 1]], axis=0
        )
        spectra = lax.dot_general(
            table_ref[core], rhs, (((1,), (1,)), ((), ())), preferred_element_type=jnp.float32
        )
        for half in range(2):
            re = spectra[:PADDED, 128 * half : 128 * half + 128]
            im = spectra[PADDED:, 128 * half : 128 * half + 128]
            power = jnp.sum(re * re + im * im, axis=1, keepdims=True)
            scaling = lax.rsqrt(power / windows + epsilon)
            re_buf[pl.ds(c + half, PADDED, stride=CH), :] = re * scaling
            im_buf[pl.ds(c + half, PADDED, stride=CH), :] = im * scaling

    @pl.loop(0, FREQS, unroll=4)
    def _(f):
        rows = pl.ds(pl.multiple_of(f * CH, CH), CH)
        white_ref[f, :, 0:128] = re_buf[rows, :].astype(jnp.bfloat16)
        white_ref[f, :, 128:256] = im_buf[rows, :].astype(jnp.bfloat16)


def spread_kernel(rows, white_ref, group_ref, halo_ref, send, recv, halo_send, halo_recv, local):
    me = lax.axis_index("cable")
    core = lax.axis_index("win")
    x, row = lax.rem(me, ROW), lax.div(me, ROW)
    base = row * ROW
    before = lax.rem(row + rows - 1, rows) * ROW + x
    after = lax.rem(row + 1, rows) * ROW + x
    peers = [base + lax.rem(x + d, ROW) for d in range(1, ROW)]
    barrier = pltpu.get_barrier_semaphore()
    for peer in [*peers, before, after]:
        pl.semaphore_signal(barrier, inc=1, device_id=(peer, core), device_id_type=MESH)
    pl.semaphore_wait(barrier, 5)

    own = pltpu.make_async_copy(white_ref.at[x], group_ref.at[x], local)
    own.start()
    copies = []
    for d in (1, 3, 2):
        copy = pltpu.make_async_remote_copy(
            src_ref=white_ref.at[lax.rem(x + d, ROW)],
            dst_ref=group_ref.at[x],
            send_sem=send.at[d],
            recv_sem=recv.at[d],
            device_id=(peers[d - 1], core),
            device_id_type=MESH,
        )
        copy.start()
        copies.append(copy)
    own.wait()
    for copy in copies:
        copy.wait()
    halos = []
    for b in range(2):
        copy = pltpu.make_async_remote_copy(
            src_ref=group_ref.at[b],
            dst_ref=halo_ref.at[b],
            send_sem=halo_send.at[b],
            recv_sem=halo_recv.at[b],
            device_id=(before, core),
            device_id_type=MESH,
        )
        copy.start()
        halos.append(copy)
    for copy in halos:
        copy.wait()


def skewed(product):
    lane = lax.broadcasted_iota(jnp.int32, (8, 128), 1)
    back = 7 - lax.broadcasted_iota(jnp.int32, (8, 128), 0)
    turned = []
    for v in range(4):
        group = jnp.take_along_axis(product[8 * v : 8 * v + 8], back, axis=0)
        shift = (120 - 8 * v + 64 * (v // 2)) % 128
        turned.append(pltpu.roll(group, shift, 1, stride=1, stride_axis=0))
    both = [jnp.where(lane < OFFS, turned[v], turned[v + 2]) for v in range(2)]
    return jnp.concatenate(both, axis=0).astype(jnp.bfloat16)


def cross_kernel(rows, group_ref, halo_ref, cross_ref):
    last = lax.div(lax.axis_index("cable"), ROW) == rows - 1

    @pl.loop(0, SLOTS, unroll=3)
    def _(f):
        blocks = [group_ref[b, f] for b in range(ROW)]
        for b in range(2):
            halo = halo_ref[b, f]
            blocks.append(jnp.where(last, jnp.zeros_like(halo), halo))
        for b in range(ROW):
            mine = blocks[b]
            flipped = jnp.concatenate([mine[:, 128:], -mine[:, :128]], axis=1)
            lhs = jnp.concatenate([mine, flipped], axis=0)
            rhs = jnp.concatenate([*blocks[b : b + 3], mine], axis=0)
            product = lax.dot_general(
                lhs, rhs, (((1,), (1,)), ((), ())), preferred_element_type=jnp.float32
            )
            for part in range(2):
                cross_ref[b, 2 * f + part] = skewed(product[32 * part : 32 * part + 32])


def gather_kernel(cross_ref, out_ref, send, recv, local):
    me = lax.axis_index("cable")
    core = lax.axis_index("win")
    x, row = lax.rem(me, ROW), lax.div(me, ROW)
    base = row * ROW
    peers = [base + lax.rem(x + d, ROW) for d in range(1, ROW)]
    barrier = pltpu.get_barrier_semaphore()
    for peer in peers:
        pl.semaphore_signal(barrier, inc=1, device_id=(peer, core), device_id_type=MESH)
    pl.semaphore_wait(barrier, 3)
    own = pltpu.make_async_copy(cross_ref.at[x], out_ref.at[x], local)
    own.start()
    copies = []
    for d in (1, 3, 2):
        copy = pltpu.make_async_remote_copy(
            src_ref=cross_ref.at[lax.rem(x + d, ROW)],
            dst_ref=out_ref.at[x],
            send_sem=send.at[d],
            recv_sem=recv.at[d],
            device_id=(peers[d - 1], core),
            device_id_type=MESH,
        )
        copy.start()
        copies.append(copy)
    own.wait()
    for copy in copies:
        copy.wait()


def back_kernel(cross_ref, inverse_ref, out_ref, buf):
    core = lax.axis_index("win")
    terms = 2 * FREQS

    @pl.loop(0, terms, unroll=8)
    def _(g):
        buf[pl.ds(g, 16, stride=terms), :] = cross_ref[g].astype(jnp.float32)

    @pl.loop(0, 16, unroll=2)
    def _(p):
        c = 8 * (p // 8) + 7 - p % 8
        spectrum = buf[pl.ds(pl.multiple_of(p * terms, 8), terms), :].astype(jnp.bfloat16)
        lags = lax.dot_general(
            spectrum,
            inverse_ref[core],
            (((0,), (0,)), ((), ())),
            preferred_element_type=jnp.float32,
        )
        out_ref[c] = lags[:OFFS]
        out_ref[c + 16] = lags[OFFS:]


VMEM = pl.BlockSpec(memory_space=pltpu.VMEM)
ANY = pl.BlockSpec(memory_space=pl.ANY)


def body(rows, records):
    samples, channels, windows = records.shape
    assert (samples, channels) == (SAMPLES, CH)
    total_windows = 2 * windows
    core = lax.axis_index("win")
    own = jnp.transpose(records, (1, 2, 0))
    other = lax.ppermute(own, "win", [(0, 1), (1, 0)])
    tables = np.stack([forward_table(0), forward_table(1)])
    factor = 1.0 / math.sqrt(2.0 * total_windows * (samples // 2 + 1))
    inverses = np.stack([inverse_table(0, factor), inverse_table(1, factor)])
    bf16 = jnp.bfloat16
    white = pl.pallas_call(
        functools.partial(whiten_kernel, total_windows),
        out_shape=jax.ShapeDtypeStruct((FREQS, CH, 256), bf16),
        in_specs=[VMEM] * 3,
        out_specs=VMEM,
        scratch_shapes=[pltpu.VMEM((PADDED * CH, 128), jnp.float32)] * 2,
        name="whiten",
    )(tables, own, other)
    white = white.reshape(ROW, SLOTS, CH, 256)
    group, halo = pl.pallas_call(
        functools.partial(spread_kernel, rows),
        out_shape=[
            jax.ShapeDtypeStruct((ROW, SLOTS, CH, 256), bf16),
            jax.ShapeDtypeStruct((2, SLOTS, CH, 256), bf16),
        ],
        in_specs=[ANY],
        out_specs=[ANY, ANY],
        scratch_shapes=[
            pltpu.SemaphoreType.DMA((4,)),
            pltpu.SemaphoreType.DMA((4,)),
            pltpu.SemaphoreType.DMA((2,)),
            pltpu.SemaphoreType.DMA((2,)),
            pltpu.SemaphoreType.DMA,
        ],
        compiler_params=pltpu.CompilerParams(collective_id=0, has_side_effects=True),
        name="spread",
    )(white)
    cross = pl.pallas_call(
        functools.partial(cross_kernel, rows),
        out_shape=jax.ShapeDtypeStruct((ROW, 2 * SLOTS, 16, 128), bf16),
        in_specs=[VMEM] * 2,
        out_specs=VMEM,
        name="cross",
    )(group, halo)
    spectrum = pl.pallas_call(
        gather_kernel,
        out_shape=jax.ShapeDtypeStruct((ROW, 2 * SLOTS, 16, 128), bf16),
        in_specs=[ANY],
        out_specs=ANY,
        scratch_shapes=[
            pltpu.SemaphoreType.DMA((4,)),
            pltpu.SemaphoreType.DMA((4,)),
            pltpu.SemaphoreType.DMA,
        ],
        compiler_params=pltpu.CompilerParams(collective_id=1, has_side_effects=True),
        name="gather",
    )(cross)
    spectrum = spectrum.reshape(2 * FREQS, 16, 128)
    half = pl.pallas_call(
        back_kernel,
        out_shape=jax.ShapeDtypeStruct((CH, OFFS, LAGS), jnp.float32),
        in_specs=[VMEM] * 2,
        out_specs=VMEM,
        scratch_shapes=[pltpu.VMEM((16 * 2 * FREQS, 128), jnp.float32)],
        name="back",
    )(spectrum, inverses)
    theirs = lax.ppermute(half.astype(bf16), "win", [(0, 1), (1, 0)]).astype(jnp.float32)
    return jnp.where(core == 0, half, -half) + theirs


def solution(mesh):
    rows = mesh.shape["cable"] // ROW
    return jax.shard_map(
        functools.partial(body, rows),
        mesh=mesh,
        in_specs=(P(None, "cable", "win"),),
        out_specs=P("cable", None, "win"),
        check_vma=False,
    )
```

time: 243 us -> 121 us (0.50)
  the two profiles are of different devices: /device:TPU:255 before, /device:TPU:1 now
where the time goes in v1:
time: 121 us
  Pallas kernels  95.4 us (79%)
  starting transfers between devices  13.3 us (11%)
  waiting for transfers between devices  6.37 us (5%)
  other arithmetic  4.76 us (4%)
  local copies, waits for them, and re-layouts  1.32 us (1%)
    pallas_call x1, Pallas kernels, body(): pl.pallas_call(functools.partial(spread_kernel, rows), out_shape=[jax.Sha...  56.4 us
    pallas_call x1, Pallas kernels, body(): pl.pallas_call(gather_kernel, out_shape=jax.ShapeDtypeStruct((ROW, 2 * SL...  14.6 us
    pallas_call x1, Pallas kernels, body(): pl.pallas_call(functools.partial(whiten_kernel, total_windows), out_shape...  11 us
    ppermute x1, starting transfers between devices, body(): other = lax.ppermute(own, 'win', [(0, 1), (1, 0)])  8.73 us
    pallas_call x1, Pallas kernels, body(): pl.pallas_call(functools.partial(cross_kernel, rows), out_shape=jax.Shape...  8.05 us
    pallas_call x1, Pallas kernels, body(): pl.pallas_call(back_kernel, out_shape=jax.ShapeDtypeStruct((CH, OFFS, LAG...  5.27 us
    ppermute x1, starting transfers between devices, body(): lax.ppermute(half.astype(bf16), 'win', [(0, 1), (1, 0)]).astype(jnp.float32)  4.58 us
    ppermute x1, waiting for transfers between devices, body(): other = lax.ppermute(own, 'win', [(0, 1), (1, 0)])  3.97 us
  transfers between devices with their start and end apart: 2, of which 2 were waited for; matrix products, arithmetic and copies ran while one was open for 0% of the time, Pallas kernels for 0%

profile of v1, /device:TPU:1, one launch (start us, length us, event | category | flops | bytes accessed | tf_op | source)
XLA Modules:
  0.0 121.2 jit_solution(16232528941145163659)
XLA Ops:
  0.0 8.7 %collective-permute-start = (bf16[32,64,512]{2,1,0:T(8,128)(2,1)}, bf16[32,64,512]{2,1,0:T(8,128)(2,1)S(1)}, u32[]{:S(2)}, u32[]{:S(2)}) collective-permute-start(bf16[32,64,512]{2,1,0:T(8,128)(2,1)} %bitcast.5), channel_id=1, source_target_pairs={{0,1},{1,0},{2,3},{3,2},{4,5},{5,4},{6,7},{7,6},{8,9},{9,8},{10,11... | collective-permute-start | bytes 6291464 | tf_op jit(solution)/shard_map/ppermute | solution.py:225
  8.7 4.0 %collective-permute-done.other_ref = bf16[32,64,512]{2,1,0:T(8,128)(2,1)S(1)} collective-permute-done((bf16[32,64,512]{2,1,0:T(8,128)(2,1)}, bf16[32,64,512]{2,1,0:T(8,128)(2,1)S(1)}, u32[]{:S(2)}, u32[]{:S(2)}) %collective-permute-start) | collective-permute-done | bytes 2097184 | tf_op jit(solution)/shard_map/ppermute | solution.py:225
  12.7 0.0 copy-start.1
  12.7 1.3 %copy-done.1 = bf16[32,64,512]{2,1,0:T(8,128)(2,1)} copy-done((bf16[32,64,512]{2,1,0:T(8,128)(2,1)}, bf16[32,64,512]{2,1,0:T(8,128)(2,1)S(1)}, u32[]{:S(2)}) %copy-start.1) | copy-done | bytes 2097176
  14.0 11.0 %whiten.1 = bf16[132,32,256]{2,1,0:T(8,128)(2,1)} custom-call(bf16[2,272,512]{2,1,0:T(8,128)(2,1)} %constant.10.clone.table_ref, bf16[32,64,512]{2,1,0:T(8,128)(2,1)} %bitcast.6, bf16[32,64,512]{2,1,0:T(8,128)(2,1)} %copy-done.1), custom_call_target="tpu_custom_call" | custom-call | tf_op jit(solution)/shard_map/whiten/pallas_call | solution.py:230
  25.1 56.4 %spread.1 = (bf16[4,33,32,256]{3,2,1,0:T(8,128)(2,1)}, bf16[2,33,32,256]{3,2,1,0:T(8,128)(2,1)}) custom-call(bf16[4,33,32,256]{3,2,1,0:T(8,128)(2,1)} %bitcast.3), custom_call_target="tpu_custom_call" | custom-call | tf_op jit(solution)/shard_map/spread/pallas_call | solution.py:239
  81.5 8.0 %cross.1.cross_ref = bf16[4,66,16,128]{3,2,1,0:T(8,128)(2,1)} custom-call(bf16[4,33,32,256]{3,2,1,0:T(8,128)(2,1)} %get-tuple-element.7.group_ref, bf16[2,33,32,256]{3,2,1,0:T(8,128)(2,1)} %get-tuple-element.8.halo_ref), custom_call_target="tpu_custom_call" | custom-call | tf_op jit(solution)/shard_map/cross/pallas_call | solution.py:257
  89.5 14.6 %gather.1 = bf16[4,66,16,128]{3,2,1,0:T(8,128)(2,1)} custom-call(bf16[4,66,16,128]{3,2,1,0:T(8,128)(2,1)} %cross.1.cross_ref), custom_call_target="tpu_custom_call" | custom-call | tf_op jit(solution)/shard_map/gather/pallas_call | solution.py:264
  104.1 5.3 %back.1 = f32[32,64,256]{2,1,0:T(8,128)} custom-call(bf16[264,16,128]{2,1,0:T(8,128)(2,1)} %bitcast.4, bf16[2,264,256]{2,1,0:T(8,128)(2,1)} %constant.11.clone.inverse_ref), custom_call_target="tpu_custom_call" | custom-call | tf_op jit(solution)/shard_map/back/pallas_call | solution.py:278
  109.4 0.0 copy-start
  109.4 1.9 %convert_element_type.6 = bf16[32,64,256]{2,1,0:T(8,128)(2,1)S(1)} convert(f32[32,64,256]{2,1,0:T(8,128)} %back.1) | non-fusion elementwise | flops 524288 | bytes 3145728 | tf_op jit(solution)/shard_map/convert_element_type | solution.py:286
  111.3 4.6 %collective-permute-start.1 = (bf16[32,64,256]{2,1,0:T(8,128)(2,1)S(1)}, bf16[32,64,256]{2,1,0:T(8,128)(2,1)}, u32[]{:S(2)}, u32[]{:S(2)}) collective-permute-start(bf16[32,64,256]{2,1,0:T(8,128)(2,1)S(1)} %convert_element_type.6), channel_id=1, source_target_pairs={{0,1},{1,0},{2,3},{3,2},{4,5},{5,4},{6,7},{7,6},{8,9},{9,8},{10,11... | collective-permute-start | bytes 3145736 | tf_op jit(solution)/shard_map/ppermute | solution.py:286
  115.9 2.4 %collective-permute-done.1 = bf16[32,64,256]{2,1,0:T(8,128)(2,1)} collective-permute-done((bf16[32,64,256]{2,1,0:T(8,128)(2,1)S(1)}, bf16[32,64,256]{2,1,0:T(8,128)(2,1)}, u32[]{:S(2)}, u32[]{:S(2)}) %collective-permute-start.1) | collective-permute-done | bytes 1048608 | tf_op jit(solution)/shard_map/ppermute | solution.py:286
  118.3 0.0 copy-done
  118.3 2.9 %fusion = f32[32,64,256]{2,1,0:T(8,128)} fusion(f32[32,64,256]{2,1,0:T(8,128)S(1)} %copy-done, bf16[32,64,256]{2,1,0:T(8,128)(2,1)} %collective-permute-done.1, pred[]{:T(512)S(6)} %eq.3), kind=kLoop, calls=%fused_computation.1 | loop fusion | flops 2097152 | bytes 5242881 | tf_op jit(solution)/shard_map/add | solution.py:287
Async XLA Ops:
  0.0 12.7 %collective-permute-start = (bf16[32,64,512]{2,1,0:T(8,128)(2,1)}, bf16[32,64,512]{2,1,0:T(8,128)(2,1)S(1)}, u32[]{:S(2)}, u32[]{:S(2)}) collective-permute-start(bf16[32,64,512]{2,1,0:T(8,128)(2,1)} %bitcast.5), channel_id=1, source_target_pairs={{0,1},{1,0},{2,3},{3,2},{4,5},{5,4},{6,7},{7,6},{8,9},{9,8},{10,11... | collective-permute-start | bytes 6291464 | tf_op jit(solution)/shard_map/ppermute | solution.py:225
  12.7 1.3 %copy-start.1 = (bf16[32,64,512]{2,1,0:T(8,128)(2,1)}, bf16[32,64,512]{2,1,0:T(8,128)(2,1)S(1)}, u32[]{:S(2)}) copy-start(bf16[32,64,512]{2,1,0:T(8,128)(2,1)S(1)} %collective-permute-done.other_ref) | copy-start | bytes 6291460
  109.4 8.9 %copy-start = (f32[32,64,256]{2,1,0:T(8,128)S(1)}, f32[32,64,256]{2,1,0:T(8,128)}, u32[]{:S(2)}) copy-start(f32[32,64,256]{2,1,0:T(8,128)} %back.1) | copy-start | bytes 6291460
  111.3 7.0 %collective-permute-start.1 = (bf16[32,64,256]{2,1,0:T(8,128)(2,1)S(1)}, bf16[32,64,256]{2,1,0:T(8,128)(2,1)}, u32[]{:S(2)}, u32[]{:S(2)}) collective-permute-start(bf16[32,64,256]{2,1,0:T(8,128)(2,1)S(1)} %convert_element_type.6), channel_id=1, source_target_pairs={{0,1},{1,0},{2,3},{3,2},{4,5},{5,4},{6,7},{7,6},{8,9},{9,8},{10,11... | collective-permute-start | bytes 3145736 | tf_op jit(solution)/shard_map/ppermute | solution.py:286

commit v2 on v0

v2 whole, which is shorter than its diff:
```python
import functools
import math

import jax
import jax.numpy as jnp
import numpy as np
from jax import lax
from jax.experimental import pallas as pl
from jax.experimental.pallas import tpu as pltpu
from jax.sharding import PartitionSpec as P

MESH = pl.DeviceIdType.MESH

OFFS = 64
SAMPLES = 512
CH = 32
ROW = 4
CHUNKS = 3
PART = 11
FREQS = ROW * PART
PADDED = 48
TERMS = 2 * FREQS
LAGS = 256
PIECES = 4

epsilon = 1e-06


def chunk_frequencies(parity, chunk):
    place = np.arange(PADDED)
    chip, slot = place // PART, chunk * PART + place % PART
    half = np.where(slot < 32, 32 * chip + slot, 128)
    held = np.where(slot < 32, chip < ROW, (chip == ROW - 1) & (parity == 0))
    return (2 * half + parity)[:, None], held[:, None]


def angles(freq, times):
    return np.float32(2.0 * math.pi / SAMPLES) * (freq * times % SAMPLES).astype(np.float32)


def forward_table(parity, chunk):
    freq, held = chunk_frequencies(parity, chunk)
    times = np.arange(SAMPLES)[None, :]
    phase = angles(freq, times)
    taper = np.float32(0.5) - np.float32(0.5) * np.cos(angles(1, times))
    taper = np.where(held, taper, np.float32(0.0))
    both = np.concatenate([taper * np.cos(phase), -taper * np.sin(phase)], axis=0)
    return both.astype(jnp.bfloat16)


def inverse_table(parity, chunk, factor):
    freq, held = chunk_frequencies(parity, chunk)
    freq, held = freq[:FREQS], held[:FREQS]
    phase = angles(freq, np.arange(LAGS)[None, :])
    weight = np.where((freq == 0) | (freq == SAMPLES // 2), 1.0, 2.0) * held * factor
    weight = weight.astype(np.float32)
    both = np.stack([weight * np.cos(phase), -weight * np.sin(phase)], axis=1)
    return both.reshape(TERMS, LAGS).astype(jnp.bfloat16)


def skewed(product):
    lane = lax.broadcasted_iota(jnp.int32, (8, 128), 1)
    back = 7 - lax.broadcasted_iota(jnp.int32, (8, 128), 0)
    turned = []
    for v in range(4):
        group = jnp.take_along_axis(product[8 * v : 8 * v + 8], back, axis=0)
        shift = (120 - 8 * v + 64 * (v // 2)) % 128
        turned.append(pltpu.roll(group, shift, 1, stride=1, stride_axis=0))
    both = [jnp.where(lane < OFFS, turned[v], turned[v + 2]) for v in range(2)]
    return jnp.concatenate(both, axis=0).astype(jnp.bfloat16)


def kernel(
    rows,
    windows,
    table_ref,
    inverse_ref,
    own_ref,
    out_ref,
    other,
    re_buf,
    im_buf,
    white,
    group,
    relayed,
    halo,
    cross,
    cross_relayed,
    back,
    turned,
    mine_out,
    theirs_in,
    pair_send,
    pair_recv,
    white_send,
    white_recv,
    relay_recv,
    forward_send,
    halo_send,
    halo_recv,
    cross_send,
    cross_recv,
    cross_relay_recv,
    cross_forward_send,
    out_send,
    out_recv,
):
    me = lax.axis_index("cable")
    core = lax.axis_index("win")
    x, row = lax.rem(me, ROW), lax.div(me, ROW)
    base = row * ROW

    def chip(distance):
        return lax.rem(x + distance, ROW)

    around = 1 + 2 * core
    opposite = 4 - around
    before = lax.rem(row + rows - 1, rows) * ROW + x
    after = lax.rem(row + 1, rows) * ROW + x
    partner = (me, 1 - core)
    barrier = pltpu.get_barrier_semaphore()
    for device in [
        partner,
        (base + chip(1), core),
        (base + chip(3), core),
        (before, core),
        (after, core),
    ]:
        pl.semaphore_signal(barrier, inc=1, device_id=device, device_id_type=MESH)
    pl.semaphore_wait(barrier, 5)

    sent = []

    def send(source, target, send_sem, recv_sem, device):
        copy = pltpu.make_async_remote_copy(
            src_ref=source,
            dst_ref=target,
            send_sem=send_sem,
            recv_sem=recv_sem,
            device_id=device,
            device_id_type=MESH,
        )
        copy.start()
        sent.append(copy)
        return copy

    def arrived(target, sem):
        pltpu.make_async_copy(target, target, sem).wait()

    def spread(source, target, relay, sends, recvs, relay_sem):
        relay_to = (base + chip(around), core)
        send(source.at[chip(2)], relay, sends.at[2], relay_sem, relay_to)
        for distance in (1, 3):
            send(
                source.at[chip(distance)],
                target.at[x],
                sends.at[distance],
                recvs.at[4 - distance],
                (base + chip(distance), core),
            )
        pltpu.make_async_copy(source.at[x], target.at[x], recvs.at[0]).start()

    def forward(target, relay, send_sem, recvs, relay_sem):
        arrived(relay, relay_sem)
        send(
            relay,
            target.at[chip(opposite)],
            send_sem,
            recvs.at[2],
            (base + chip(around), core),
        )

    eighth = CH // PIECES
    exchange = []
    for q in range(PIECES):
        piece = pl.ds(q * eighth, eighth)
        copy = send(
            own_ref.at[piece], other.at[piece], pair_send.at[q], pair_recv.at[q], partner
        )
        exchange.append(copy)

    def whiten(j):
        def pair_of_channels(c):
            rhs = jnp.concatenate(
                [own_ref[c], other[c], own_ref[c + 1], other[c + 1]], axis=0
            )
            spectra = lax.dot_general(
                table_ref[core, j],
                rhs,
                (((1,), (1,)), ((), ())),
                preferred_element_type=jnp.float32,
            )
            for half in range(2):
                re = spectra[:PADDED, 128 * half : 128 * half + 128]
                im = spectra[PADDED:, 128 * half : 128 * half + 128]
                power = jnp.sum(re * re + im * im, axis=1, keepdims=True)
                scaling = lax.rsqrt(power / windows + epsilon)
                re_buf[pl.ds(c + half, PADDED, stride=CH), :] = re * scaling
                im_buf[pl.ds(c + half, PADDED, stride=CH), :] = im * scaling

        for q in range(PIECES):
            if j == 0:
                exchange[q].wait_recv()

            @pl.loop(0, eighth // 2, unroll=2)
            def _(pair):
                pair_of_channels(q * eighth + 2 * pair)

        for b in range(ROW):

            @pl.loop(0, PART)
            def _(f):
                here = pl.ds(pl.multiple_of((b * PART + f) * CH, CH), CH)
                white[j, b, f, :, 0:128] = re_buf[here, :].astype(jnp.bfloat16)
                white[j, b, f, :, 128:256] = im_buf[here, :].astype(jnp.bfloat16)

        spread(
            white.at[j],
            group.at[j],
            relayed.at[j],
            white_send.at[j],
            white_recv.at[j],
            relay_recv.at[j],
        )

    def forward_white(j):
        forward(
            group.at[j], relayed.at[j], forward_send.at[j], white_recv.at[j], relay_recv.at[j]
        )

    halos = {}

    def send_halo(j):
        for b in range(2):
            arrived(group.at[j, b], white_recv.at[j, lax.rem(b + ROW - x, ROW)])
            halos[j, b] = send(
                group.at[j, b],
                halo.at[j, b],
                halo_send.at[j, b],
                halo_recv.at[j, b],
                (before, core),
            )

    last = row == rows - 1

    def correlate(j):
        for b in range(2, ROW):
            arrived(group.at[j, b], white_recv.at[j, lax.rem(b + ROW - x, ROW)])
        for b in range(2):
            halos[j, b].wait_recv()

        @pl.loop(0, PART)
        def _(f):
            blocks = [group[j, b, f] for b in range(ROW)]
            for b in range(2):
                there = halo[j, b, f]
                blocks.append(jnp.where(last, jnp.zeros_like(there), there))
            for b in range(ROW):
                mine = blocks[b]
                flipped = jnp.concatenate([mine[:, 128:], -mine[:, :128]], axis=1)
                lhs = jnp.concatenate([mine, flipped], axis=0)
                rhs = jnp.concatenate([*blocks[b : b + 3], mine], axis=0)
                product = lax.dot_general(
                    lhs, rhs, (((1,), (1,)), ((), ())), preferred_element_type=jnp.float32
                )
                for part in range(2):
                    cross[j, b, 2 * f + part] = skewed(product[32 * part : 32 * part + 32])

        spread(
            cross.at[j],
            back.at[j],
            cross_relayed.at[j],
            cross_send.at[j],
            cross_recv.at[j],
            cross_relay_recv.at[j],
        )

    def forward_cross(j):
        forward(
            back.at[j],
            cross_relayed.at[j],
            cross_forward_send.at[j],
            cross_recv.at[j],
            cross_relay_recv.at[j],
        )

    def turn(j):
        for b in range(ROW):
            arrived(back.at[j, b], cross_recv.at[j, lax.rem(b + ROW - x, ROW)])
        for b in range(ROW):

            @pl.loop(0, 2 * PART, unroll=2)
            def _(g):
                place = (j * ROW + b) * 2 * PART + g
                turned[pl.ds(place, 16, stride=CHUNKS * TERMS), :] = back[j, b, g].astype(
                    jnp.float32
                )

    whiten(0)
    whiten(1)
    whiten(2)
    forward_white(0)
    send_halo(0)
    forward_white(1)
    send_halo(1)
    forward_white(2)
    correlate(0)
    send_halo(2)
    correlate(1)
    forward_cross(0)
    turn(0)
    correlate(2)
    forward_cross(1)
    forward_cross(2)
    turn(1)
    turn(2)

    outs = []
    quarter = 16 // PIECES
    for q in range(PIECES):

        @pl.loop(q * quarter, (q + 1) * quarter, unroll=2)
        def _(p):
            c = 8 * (p // 8) + 7 - p % 8
            here = pl.ds(pl.multiple_of(p * CHUNKS * TERMS, 8), CHUNKS * TERMS)
            lags = lax.dot_general(
                turned[here, :].astype(jnp.bfloat16),
                inverse_ref[core],
                (((0,), (0,)), ((), ())),
                preferred_element_type=jnp.float32,
            )
            mine_out[p] = lags.astype(jnp.bfloat16)
            out_ref[c] = lags[:OFFS]
            out_ref[c + 16] = lags[OFFS:]

        piece = pl.ds(q * quarter, quarter)
        outs.append(
            send(mine_out.at[piece], theirs_in.at[piece], out_send.at[q], out_recv.at[q], partner)
        )

    sign = (1 - 2 * core).astype(jnp.float32)
    for q in range(PIECES):
        outs[q].wait_recv()

        @pl.loop(q * quarter, (q + 1) * quarter)
        def _(p):
            c = 8 * (p // 8) + 7 - p % 8
            theirs = theirs_in[p].astype(jnp.float32)
            out_ref[c] = sign * out_ref[c] + theirs[:OFFS]
            out_ref[c + 16] = sign * out_ref[c + 16] + theirs[OFFS:]

    for copy in sent:
        copy.wait_send()


VMEM = pl.BlockSpec(memory_space=pltpu.VMEM)


def body(rows, records):
    samples, channels, windows = records.shape
    assert (samples, channels) == (SAMPLES, CH)
    total_windows = 2 * windows
    own = jnp.transpose(records, (1, 2, 0))
    tables = np.stack(
        [[forward_table(parity, chunk) for chunk in range(CHUNKS)] for parity in range(2)]
    )
    factor = 1.0 / math.sqrt(2.0 * total_windows * (samples // 2 + 1))
    inverses = np.stack(
        [
            np.concatenate([inverse_table(parity, chunk, factor) for chunk in range(CHUNKS)])
            for parity in range(2)
        ]
    )
    bf16, f32 = jnp.bfloat16, jnp.float32
    dma = pltpu.SemaphoreType.DMA
    return pl.pallas_call(
        functools.partial(kernel, rows, total_windows),
        out_shape=jax.ShapeDtypeStruct((CH, OFFS, LAGS), f32),
        in_specs=[VMEM] * 3,
        out_specs=VMEM,
        scratch_shapes=[
            pltpu.VMEM((CH, windows, SAMPLES), bf16),
            pltpu.VMEM((PADDED * CH, 128), f32),
            pltpu.VMEM((PADDED * CH, 128), f32),
            pltpu.VMEM((CHUNKS, ROW, PART, CH, 256), bf16),
            pltpu.VMEM((CHUNKS, ROW, PART, CH, 256), bf16),
            pltpu.VMEM((CHUNKS, PART, CH, 256), bf16),
            pltpu.VMEM((CHUNKS, 2, PART, CH, 256), bf16),
            pltpu.VMEM((CHUNKS, ROW, 2 * PART, 16, 128), bf16),
            pltpu.VMEM((CHUNKS, 2 * PART, 16, 128), bf16),
            pltpu.VMEM((CHUNKS, ROW, 2 * PART, 16, 128), bf16),
            pltpu.VMEM((16 * CHUNKS * TERMS, 128), f32),
            pltpu.VMEM((16, 2 * OFFS, LAGS), bf16),
            pltpu.VMEM((16, 2 * OFFS, LAGS), bf16),
            dma((PIECES,)),
            dma((PIECES,)),
            dma((CHUNKS, 4)),
            dma((CHUNKS, 4)),
            dma((CHUNKS,)),
            dma((CHUNKS,)),
            dma((CHUNKS, 2)),
            dma((CHUNKS, 2)),
            dma((CHUNKS, 4)),
            dma((CHUNKS, 4)),
            dma((CHUNKS,)),
            dma((CHUNKS,)),
            dma((PIECES,)),
            dma((PIECES,)),
        ],
        compiler_params=pltpu.CompilerParams(collective_id=0, has_side_effects=True),
        name="correlate",
    )(tables, inverses, own)


def solution(mesh):
    rows = mesh.shape["cable"] // ROW
    return jax.shard_map(
        functools.partial(body, rows),
        mesh=mesh,
        in_specs=(P(None, "cable", "win"),),
        out_specs=P("cable", None, "win"),
        check_vma=False,
    )
```

time: 243 us -> 82.3 us (0.34)
  the two profiles are of different devices: /device:TPU:255 before, /device:TPU:251 now
where the time goes in v2:
time: 82.3 us; the launch traced here: 82.1 us
  Pallas kernels  79 us (96%)
  local copies, waits for them, and re-layouts  3.13 us (4%)
    pallas_call x1, Pallas kernels, body(): pl.pallas_call(functools.partial(kernel, rows, total_windows), out_shape=...  79 us
    unnamed x1, local copies, waits for them, and re-layouts  3.13 us

profile of v2, /device:TPU:251, one launch (start us, length us, event | category | flops | bytes accessed | tf_op | source)
XLA Modules:
  0.0 82.1 jit_solution(10755100548439546582)
XLA Ops:
  0.0 79.0 %correlate.1 = f32[32,64,256]{2,1,0:T(8,128)} custom-call(bf16[2,3,96,512]{3,2,1,0:T(8,128)(2,1)} %constant.4.clone.table_ref, bf16[2,264,256]{2,1,0:T(8,128)(2,1)} %constant.5.clone.inverse_ref, bf16[32,64,512]{2,1,0:T(8,128)(2,1)} %bitcast.1), custom_call_target="tpu_custom_call" | custom-call | tf_op jit(solution)/shard_map/correlate/pallas_call | solution.py:376
  79.0 3.1 %copy.5 = f32[32,64,256]{2,1,0:T(8,128)} copy(f32[32,64,256]{2,1,0:T(8,128)} %correlate.1) | data formatting | bytes 4194304

commit v3 on v2

--- a/solution.py
+++ b/solution.py
@@ -24,6 +24,7 @@
 PIECES = 4
 
 epsilon = 1e-06
+UNROLL = 4
 
 
 def chunk_frequencies(parity, chunk):
@@ -77,31 +78,25 @@
     inverse_ref,
     own_ref,
     out_ref,
+    theirs_ref,
     other,
     re_buf,
     im_buf,
     white,
     group,
-    relayed,
     halo,
     cross,
-    cross_relayed,
     back,
     turned,
     mine_out,
-    theirs_in,
     pair_send,
     pair_recv,
     white_send,
     white_recv,
-    relay_recv,
-    forward_send,
     halo_send,
     halo_recv,
     cross_send,
     cross_recv,
-    cross_relay_recv,
-    cross_forward_send,
     out_send,
     out_recv,
 ):
@@ -113,8 +108,6 @@
     def chip(distance):
         return lax.rem(x + distance, ROW)
 
-    around = 1 + 2 * core
-    opposite = 4 - around
     before = lax.rem(row + rows - 1, rows) * ROW + x
     after = lax.rem(row + 1, rows) * ROW + x
     partner = (me, 1 - core)
@@ -122,17 +115,18 @@
     for device in [
         partner,
         (base + chip(1), core),
+        (base + chip(2), core),
         (base + chip(3), core),
         (before, core),
         (after, core),
     ]:
         pl.semaphore_signal(barrier, inc=1, device_id=device, device_id_type=MESH)
-    pl.semaphore_wait(barrier, 5)
+    pl.semaphore_wait(barrier, 6)
 
     sent = []
 
-    def send(source, target, send_sem, recv_sem, device):
-        copy = pltpu.make_async_remote_copy(
+    def copy_to(source, target, send_sem, recv_sem, device):
+        return pltpu.make_async_remote_copy(
             src_ref=source,
             dst_ref=target,
             send_sem=send_sem,
@@ -140,6 +134,9 @@
             device_id=device,
             device_id_type=MESH,
         )
+
+    def send(*args):
+        copy = copy_to(*args)
         copy.start()
         sent.append(copy)
         return copy
@@ -147,10 +144,8 @@
     def arrived(target, sem):
         pltpu.make_async_copy(target, target, sem).wait()
 
-    def spread(source, target, relay, sends, recvs, relay_sem):
-        relay_to = (base + chip(around), core)
-        send(source.at[chip(2)], relay, sends.at[2], relay_sem, relay_to)
-        for distance in (1, 3):
+    def spread(source, target, sends, recvs):
+        for distance in (2, 1, 3):
             send(
                 source.at[chip(distance)],
                 target.at[x],
@@ -159,16 +154,6 @@
                 (base + chip(distance), core),
             )
         pltpu.make_async_copy(source.at[x], target.at[x], recvs.at[0]).start()
-
-    def forward(target, relay, send_sem, recvs, relay_sem):
-        arrived(relay, relay_sem)
-        send(
-            relay,
-            target.at[chip(opposite)],
-            send_sem,
-            recvs.at[2],
-            (base + chip(around), core),
-        )
 
     eighth = CH // PIECES
     exchange = []
@@ -202,7 +187,7 @@
             if j == 0:
                 exchange[q].wait_recv()
 
-            @pl.loop(0, eighth // 2, unroll=2)
+            @pl.loop(0, eighth // 2, unroll=4)
             def _(pair):
                 pair_of_channels(q * eighth + 2 * pair)
 
@@ -214,19 +199,8 @@
                 white[j, b, f, :, 0:128] = re_buf[here, :].astype(jnp.bfloat16)
                 white[j, b, f, :, 128:256] = im_buf[here, :].astype(jnp.bfloat16)
 
-        spread(
-            white.at[j],
-            group.at[j],
-            relayed.at[j],
-            white_send.at[j],
-            white_recv.at[j],
-            relay_recv.at[j],
-        )
-
-    def forward_white(j):
-        forward(
-            group.at[j], relayed.at[j], forward_send.at[j], white_recv.at[j], relay_recv.at[j]
-        )
+    def send_white(j):
+        spread(white.at[j], group.at[j], white_send.at[j], white_recv.at[j])
 
     halos = {}
 
@@ -251,38 +225,28 @@
 
         @pl.loop(0, PART)
         def _(f):
-            blocks = [group[j, b, f] for b in range(ROW)]
-            for b in range(2):
-                there = halo[j, b, f]
-                blocks.append(jnp.where(last, jnp.zeros_like(there), there))
             for b in range(ROW):
-                mine = blocks[b]
+                mine = group[j, b, f]
                 flipped = jnp.concatenate([mine[:, 128:], -mine[:, :128]], axis=1)
                 lhs = jnp.concatenate([mine, flipped], axis=0)
-                rhs = jnp.concatenate([*blocks[b : b + 3], mine], axis=0)
+                partners = []
+                for other_block in range(b, b + 3):
+                    if other_block < ROW:
+                        partners.append(group[j, other_block, f])
+                    else:
+                        there = halo[j, other_block - ROW, f]
+                        partners.append(jnp.where(last, jnp.zeros_like(there), there))
+                rhs = jnp.concatenate([*partners, mine], axis=0)
                 product = lax.dot_general(
                     lhs, rhs, (((1,), (1,)), ((), ())), preferred_element_type=jnp.float32
                 )
                 for part in range(2):
                     cross[j, b, 2 * f + part] = skewed(product[32 * part : 32 * part + 32])
 
-        spread(
-            cross.at[j],
-            back.at[j],
-            cross_relayed.at[j],
-            cross_send.at[j],
-            cross_recv.at[j],
-            cross_relay_recv.at[j],
-        )
-
-    def forward_cross(j):
-        forward(
-            back.at[j],
-            cross_relayed.at[j],
-            cross_forward_send.at[j],
-            cross_recv.at[j],
-            cross_relay_recv.at[j],
-        )
+        spread(cross.at[j], back.at[j], cross_send.at[j], cross_recv.at[j])
+
+    outs = []
+    quarter = 16 // PIECES
 
     def turn(j):
         for b in range(ROW):
@@ -291,64 +255,63 @@
 
             @pl.loop(0, 2 * PART, unroll=2)
             def _(g):
-                place = (j * ROW + b) * 2 * PART + g
-                turned[pl.ds(place, 16, stride=CHUNKS * TERMS), :] = back[j, b, g].astype(
+                turned[pl.ds(b * 2 * PART + g, 16, stride=TERMS), :] = back[j, b, g].astype(
                     jnp.float32
                 )
 
+        for q in range(PIECES):
+
+            @pl.loop(q * quarter, (q + 1) * quarter, unroll=UNROLL)
+            def _(p):
+                c = 8 * (p // 8) + 7 - p % 8
+                here = pl.ds(pl.multiple_of(p * TERMS, 8), TERMS)
+                lags = lax.dot_general(
+                    turned[here, :].astype(jnp.bfloat16),
+                    inverse_ref[core, j],
+                    (((0,), (0,)), ((), ())),
+                    preferred_element_type=jnp.float32,
+                )
+                for half in range(2):
+                    total = lags[OFFS * half : OFFS * half + OFFS]
+                    if j > 0:
+                        total = total + out_ref[c + 16 * half]
+                    out_ref[c + 16 * half] = total
+                    if j == CHUNKS - 1:
+                        mine_out[c + 16 * half] = total.astype(jnp.bfloat16)
+
+            if j == CHUNKS - 1:
+                for half in range(2):
+                    first = 8 * (q // 2) + 4 * (1 - q % 2) + 16 * half
+                    piece = pl.ds(first, quarter)
+                    place = 2 * q + half
+                    outs.append(
+                        send(
+                            mine_out.at[piece],
+                            theirs_ref.at[piece],
+                            out_send.at[place],
+                            out_recv.at[place],
+                            partner,
+                        )
+                    )
+
     whiten(0)
+    send_white(0)
     whiten(1)
+    send_white(1)
     whiten(2)
-    forward_white(0)
+    send_white(2)
     send_halo(0)
-    forward_white(1)
     send_halo(1)
-    forward_white(2)
     correlate(0)
     send_halo(2)
     correlate(1)
-    forward_cross(0)
+    correlate(2)
     turn(0)
-    correlate(2)
-    forward_cross(1)
-    forward_cross(2)
     turn(1)
     turn(2)
 
-    outs = []
-    quarter = 16 // PIECES
-    for q in range(PIECES):
-
-        @pl.loop(q * quarter, (q + 1) * quarter, unroll=2)
-        def _(p):
-            c = 8 * (p // 8) + 7 - p % 8
-            here = pl.ds(pl.multiple_of(p * CHUNKS * TERMS, 8), CHUNKS * TERMS)
-            lags = lax.dot_general(
-                turned[here, :].astype(jnp.bfloat16),
-                inverse_ref[core],
-                (((0,), (0,)), ((), ())),
-                preferred_element_type=jnp.float32,
-            )
-            mine_out[p] = lags.astype(jnp.bfloat16)
-            out_ref[c] = lags[:OFFS]
-            out_ref[c + 16] = lags[OFFS:]
-
-        piece = pl.ds(q * quarter, quarter)
-        outs.append(
-            send(mine_out.at[piece], theirs_in.at[piece], out_send.at[q], out_recv.at[q], partner)
-        )
-
-    sign = (1 - 2 * core).astype(jnp.float32)
-    for q in range(PIECES):
-        outs[q].wait_recv()
-
-        @pl.loop(q * quarter, (q + 1) * quarter)
-        def _(p):
-            c = 8 * (p // 8) + 7 - p % 8
-            theirs = theirs_in[p].astype(jnp.float32)
-            out_ref[c] = sign * out_ref[c] + theirs[:OFFS]
-            out_ref[c + 16] = sign * out_ref[c + 16] + theirs[OFFS:]
-
+    for copy in outs:
+        copy.wait_recv()
     for copy in sent:
         copy.wait_send()
 
@@ -367,49 +330,46 @@
     factor = 1.0 / math.sqrt(2.0 * total_windows * (samples // 2 + 1))
     inverses = np.stack(
         [
-            np.concatenate([inverse_table(parity, chunk, factor) for chunk in range(CHUNKS)])
+            [inverse_table(parity, chunk, factor) for chunk in range(CHUNKS)]
             for parity in range(2)
         ]
     )
     bf16, f32 = jnp.bfloat16, jnp.float32
     dma = pltpu.SemaphoreType.DMA
-    return pl.pallas_call(
+    half, theirs = pl.pallas_call(
         functools.partial(kernel, rows, total_windows),
-        out_shape=jax.ShapeDtypeStruct((CH, OFFS, LAGS), f32),
+        out_shape=[
+            jax.ShapeDtypeStruct((CH, OFFS, LAGS), f32),
+            jax.ShapeDtypeStruct((CH, OFFS, LAGS), bf16),
+        ],
         in_specs=[VMEM] * 3,
-        out_specs=VMEM,
+        out_specs=[VMEM] * 2,
         scratch_shapes=[
             pltpu.VMEM((CH, windows, SAMPLES), bf16),
             pltpu.VMEM((PADDED * CH, 128), f32),
             pltpu.VMEM((PADDED * CH, 128), f32),
             pltpu.VMEM((CHUNKS, ROW, PART, CH, 256), bf16),
             pltpu.VMEM((CHUNKS, ROW, PART, CH, 256), bf16),
-            pltpu.VMEM((CHUNKS, PART, CH, 256), bf16),
             pltpu.VMEM((CHUNKS, 2, PART, CH, 256), bf16),
             pltpu.VMEM((CHUNKS, ROW, 2 * PART, 16, 128), bf16),
-            pltpu.VMEM((CHUNKS, 2 * PART, 16, 128), bf16),
             pltpu.VMEM((CHUNKS, ROW, 2 * PART, 16, 128), bf16),
-            pltpu.VMEM((16 * CHUNKS * TERMS, 128), f32),
-            pltpu.VMEM((16, 2 * OFFS, LAGS), bf16),
-            pltpu.VMEM((16, 2 * OFFS, LAGS), bf16),
+            pltpu.VMEM((16 * TERMS, 128), f32),
+            pltpu.VMEM((CH, OFFS, LAGS), bf16),
             dma((PIECES,)),
             dma((PIECES,)),
             dma((CHUNKS, 4)),
             dma((CHUNKS, 4)),
-            dma((CHUNKS,)),
-            dma((CHUNKS,)),
             dma((CHUNKS, 2)),
             dma((CHUNKS, 2)),
             dma((CHUNKS, 4)),
             dma((CHUNKS, 4)),
-            dma((CHUNKS,)),
-            dma((CHUNKS,)),
-            dma((PIECES,)),
-            dma((PIECES,)),
+            dma((2 * PIECES,)),
+            dma((2 * PIECES,)),
         ],
         compiler_params=pltpu.CompilerParams(collective_id=0, has_side_effects=True),
         name="correlate",
     )(tables, inverses, own)
+    return jnp.where(lax.axis_index("win") == 0, half, -half) + theirs.astype(f32)
 
 
 def solution(mesh):

time: 82.3 us -> 69.5 us (0.84)
  the two profiles are of different devices: /device:TPU:251 before, /device:TPU:1 now
where the time goes in v3:
time: 69.5 us; the launch traced here: 69.4 us
  Pallas kernels  65.8 us (95%)
  other arithmetic  3.6 us (5%)
    pallas_call x1, Pallas kernels, body(): pl.pallas_call(functools.partial(kernel, rows, total_windows), out_shape=...  65.8 us
    add x1, other arithmetic, body(): jnp.where(lax.axis_index('win') == 0, half, -half) + theirs.astype(f32)  3.6 us

profile of v3, /device:TPU:1, one launch (start us, length us, event | category | flops | bytes accessed | tf_op | source)
XLA Modules:
  0.0 69.4 jit_solution(3432232012203672209)
XLA Ops:
  0.0 65.8 %correlate.1 = (f32[32,64,256]{2,1,0:T(8,128)}, bf16[32,64,256]{2,1,0:T(8,128)(2,1)}) custom-call(bf16[2,3,96,512]{3,2,1,0:T(8,128)(2,1)} %constant.10.clone.table_ref, bf16[2,3,88,256]{3,2,1,0:T(8,128)(2,1)} %constant.11.clone.inverse_ref, bf16[32,64,512]{2,1,0:T(8,128)(2,1)} %bitcast.1), custom_call_target="tpu_custom_call" | custom-call | tf_op jit(solution)/shard_map/correlate/pallas_call | solution.py:339
  65.8 3.6 %fusion = f32[32,64,256]{2,1,0:T(8,128)} fusion(f32[32,64,256]{2,1,0:T(8,128)} %get-tuple-element.7, bf16[32,64,256]{2,1,0:T(8,128)(2,1)} %get-tuple-element.8, pred[]{:T(512)S(6)} %eq.3), kind=kLoop, calls=%fused_computation.1 | loop fusion | flops 2097152 | bytes 5242881 | tf_op jit(solution)/shard_map/add | solution.py:372

commit v4 on v3

--- a/solution.py
+++ b/solution.py
@@ -77,8 +77,9 @@
     table_ref,
     inverse_ref,
     own_ref,
+    half_ref,
+    theirs_ref,
     out_ref,
-    theirs_ref,
     other,
     re_buf,
     im_buf,
@@ -88,7 +89,6 @@
     cross,
     back,
     turned,
-    mine_out,
     pair_send,
     pair_recv,
     white_send,
@@ -193,7 +193,7 @@
 
         for b in range(ROW):
 
-            @pl.loop(0, PART)
+            @pl.loop(0, PART, unroll=PART)
             def _(f):
                 here = pl.ds(pl.multiple_of((b * PART + f) * CH, CH), CH)
                 white[j, b, f, :, 0:128] = re_buf[here, :].astype(jnp.bfloat16)
@@ -223,8 +223,7 @@
         for b in range(2):
             halos[j, b].wait_recv()
 
-        @pl.loop(0, PART)
-        def _(f):
+        def frequency(f):
             for b in range(ROW):
                 mine = group[j, b, f]
                 flipped = jnp.concatenate([mine[:, 128:], -mine[:, :128]], axis=1)
@@ -243,6 +242,13 @@
                 for part in range(2):
                     cross[j, b, 2 * f + part] = skewed(product[32 * part : 32 * part + 32])
 
+        @pl.loop(0, PART // 2)
+        def _(pair):
+            frequency(2 * pair)
+            frequency(2 * pair + 1)
+
+        frequency(PART - 1)
+
         spread(cross.at[j], back.at[j], cross_send.at[j], cross_recv.at[j])
 
     outs = []
@@ -253,7 +259,7 @@
             arrived(back.at[j, b], cross_recv.at[j, lax.rem(b + ROW - x, ROW)])
         for b in range(ROW):
 
-            @pl.loop(0, 2 * PART, unroll=2)
+            @pl.loop(0, 2 * PART, unroll=PART)
             def _(g):
                 turned[pl.ds(b * 2 * PART + g, 16, stride=TERMS), :] = back[j, b, g].astype(
                     jnp.float32
@@ -275,9 +281,10 @@
                     total = lags[OFFS * half : OFFS * half + OFFS]
                     if j > 0:
                         total = total + out_ref[c + 16 * half]
-                    out_ref[c + 16 * half] = total
-                    if j == CHUNKS - 1:
-                        mine_out[c + 16 * half] = total.astype(jnp.bfloat16)
+                    if j < CHUNKS - 1:
+                        out_ref[c + 16 * half] = total
+                    else:
+                        half_ref[c + 16 * half] = total.astype(jnp.bfloat16)
 
             if j == CHUNKS - 1:
                 for half in range(2):
@@ -286,7 +293,7 @@
                     place = 2 * q + half
                     outs.append(
                         send(
-                            mine_out.at[piece],
+                            half_ref.at[piece],
                             theirs_ref.at[piece],
                             out_send.at[place],
                             out_recv.at[place],
@@ -339,12 +346,13 @@
     half, theirs = pl.pallas_call(
         functools.partial(kernel, rows, total_windows),
         out_shape=[
-            jax.ShapeDtypeStruct((CH, OFFS, LAGS), f32),
+            jax.ShapeDtypeStruct((CH, OFFS, LAGS), bf16),
             jax.ShapeDtypeStruct((CH, OFFS, LAGS), bf16),
         ],
         in_specs=[VMEM] * 3,
         out_specs=[VMEM] * 2,
         scratch_shapes=[
+            pltpu.VMEM((CH, OFFS, LAGS), f32),
             pltpu.VMEM((CH, windows, SAMPLES), bf16),
             pltpu.VMEM((PADDED * CH, 128), f32),
             pltpu.VMEM((PADDED * CH, 128), f32),
@@ -354,7 +362,6 @@
             pltpu.VMEM((CHUNKS, ROW, 2 * PART, 16, 128), bf16),
             pltpu.VMEM((CHUNKS, ROW, 2 * PART, 16, 128), bf16),
             pltpu.VMEM((16 * TERMS, 128), f32),
-            pltpu.VMEM((CH, OFFS, LAGS), bf16),
             dma((PIECES,)),
             dma((PIECES,)),
             dma((CHUNKS, 4)),
@@ -369,6 +376,7 @@
         compiler_params=pltpu.CompilerParams(collective_id=0, has_side_effects=True),
         name="correlate",
     )(tables, inverses, own)
+    half = half.astype(f32)
     return jnp.where(lax.axis_index("win") == 0, half, -half) + theirs.astype(f32)
 
 

time: 69.5 us -> 67.5 us (0.971)
  Pallas kernels: 65.8 us -> 64.1 us
    pallas_call x1, Pallas kernels: 65.8 us -> 64.1 us  [body(): pl.pallas_call(functools.partial(kernel, rows, total_windows), out_shape=...]
where the time goes in v4:
time: 67.5 us; the launch traced here: 67.3 us
  Pallas kernels  64.1 us (95%)
  other arithmetic  3.28 us (5%)
    pallas_call x1, Pallas kernels, body(): pl.pallas_call(functools.partial(kernel, rows, total_windows), out_shape=...  64.1 us
    add x1, other arithmetic, body(): jnp.where(lax.axis_index('win') == 0, half, -half) + theirs.astype(f32)  3.28 us

profile of v4, /device:TPU:1, one launch (start us, length us, event | category | flops | bytes accessed | tf_op | source)
XLA Modules:
  0.0 67.3 jit_solution(14428168277784372658)
XLA Ops:
  0.0 64.1 %correlate.1 = (bf16[32,64,256]{2,1,0:T(8,128)(2,1)}, bf16[32,64,256]{2,1,0:T(8,128)(2,1)}) custom-call(bf16[2,3,96,512]{3,2,1,0:T(8,128)(2,1)} %constant.10.clone.table_ref, bf16[2,3,88,256]{3,2,1,0:T(8,128)(2,1)} %constant.11.clone.inverse_ref, bf16[32,64,512]{2,1,0:T(8,128)(2,1)} %bitcast.1), custom_call_target="tpu_custom_call" | custom-call | tf_op jit(solution)/shard_map/correlate/pallas_call | solution.py:346
  64.1 3.3 %fusion = f32[32,64,256]{2,1,0:T(8,128)} fusion(bf16[32,64,256]{2,1,0:T(8,128)(2,1)} %get-tuple-element.8, bf16[32,64,256]{2,1,0:T(8,128)(2,1)} %get-tuple-element.7, pred[]{:T(512)S(6)} %eq.3), kind=kLoop, calls=%fused_computation.1 | loop fusion | flops 2621440 | bytes 4194305 | tf_op jit(solution)/shard_map/add | solution.py:380

commit v5 on v4

--- a/solution.py
+++ b/solution.py
@@ -21,6 +21,7 @@
 PADDED = 48
 TERMS = 2 * FREQS
 LAGS = 256
+SPANS = ((0, 6), (6, 5))
 PIECES = 4
 
 epsilon = 1e-06
@@ -217,6 +218,10 @@
 
     last = row == rows - 1
 
+    def of_span(ref, span):
+        first, size = SPANS[span]
+        return ref.at[:, pl.ds(2 * first, 2 * size)]
+
     def correlate(j):
         for b in range(2, ROW):
             arrived(group.at[j, b], white_recv.at[j, lax.rem(b + ROW - x, ROW)])
@@ -242,28 +247,39 @@
                 for part in range(2):
                     cross[j, b, 2 * f + part] = skewed(product[32 * part : 32 * part + 32])
 
-        @pl.loop(0, PART // 2)
-        def _(pair):
-            frequency(2 * pair)
-            frequency(2 * pair + 1)
-
-        frequency(PART - 1)
-
-        spread(cross.at[j], back.at[j], cross_send.at[j], cross_recv.at[j])
+        for span, (first, size) in enumerate(SPANS):
+
+            @pl.loop(0, size // 2)
+            def _(pair):
+                frequency(first + 2 * pair)
+                frequency(first + 2 * pair + 1)
+
+            if size % 2:
+                frequency(first + size - 1)
+            spread(
+                of_span(cross.at[j], span),
+                of_span(back.at[j], span),
+                cross_send.at[j, span],
+                cross_recv.at[j, span],
+            )
 
     outs = []
     quarter = 16 // PIECES
 
     def turn(j):
-        for b in range(ROW):
-            arrived(back.at[j, b], cross_recv.at[j, lax.rem(b + ROW - x, ROW)])
-        for b in range(ROW):
-
-            @pl.loop(0, 2 * PART, unroll=PART)
-            def _(g):
-                turned[pl.ds(b * 2 * PART + g, 16, stride=TERMS), :] = back[j, b, g].astype(
-                    jnp.float32
+        for span, (first, size) in enumerate(SPANS):
+            for b in range(ROW):
+                arrived(
+                    back.at[j, b, pl.ds(2 * first, 2 * size)],
+                    cross_recv.at[j, span, lax.rem(b + ROW - x, ROW)],
                 )
+            for b in range(ROW):
+
+                @pl.loop(2 * first, 2 * (first + size), unroll=2 * size)
+                def _(g):
+                    turned[pl.ds(b * 2 * PART + g, 16, stride=TERMS), :] = back[j, b, g].astype(
+                        jnp.float32
+                    )
 
         for q in range(PIECES):
 
@@ -368,8 +384,8 @@
             dma((CHUNKS, 4)),
             dma((CHUNKS, 2)),
             dma((CHUNKS, 2)),
-            dma((CHUNKS, 4)),
-            dma((CHUNKS, 4)),
+            dma((CHUNKS, len(SPANS), 4)),
+            dma((CHUNKS, len(SPANS), 4)),
             dma((2 * PIECES,)),
             dma((2 * PIECES,)),
         ],

time: 67.5 us -> 67.3 us (level)
  no operation moved by 1% of the time
where the time goes in v5:
time: 67.3 us; the launch traced here: 67.2 us
  Pallas kernels  63.9 us (95%)
  other arithmetic  3.28 us (5%)
    pallas_call x1, Pallas kernels, body(): pl.pallas_call(functools.partial(kernel, rows, total_windows), out_shape=...  63.9 us
    add x1, other arithmetic, body(): jnp.where(lax.axis_index('win') == 0, half, -half) + theirs.astype(f32)  3.28 us

profile of v5, /device:TPU:1, one launch (start us, length us, event | category | flops | bytes accessed | tf_op | source)
XLA Modules:
  0.0 67.2 jit_solution(6459099792855373260)
XLA Ops:
  0.0 63.9 %correlate.1 = (bf16[32,64,256]{2,1,0:T(8,128)(2,1)}, bf16[32,64,256]{2,1,0:T(8,128)(2,1)}) custom-call(bf16[2,3,96,512]{3,2,1,0:T(8,128)(2,1)} %constant.10.clone.table_ref, bf16[2,3,88,256]{3,2,1,0:T(8,128)(2,1)} %constant.11.clone.inverse_ref, bf16[32,64,512]{2,1,0:T(8,128)(2,1)} %bitcast.1), custom_call_target="tpu_custom_call" | custom-call | tf_op jit(solution)/shard_map/correlate/pallas_call | solution.py:362
  63.9 3.3 %fusion = f32[32,64,256]{2,1,0:T(8,128)} fusion(bf16[32,64,256]{2,1,0:T(8,128)(2,1)} %get-tuple-element.8, bf16[32,64,256]{2,1,0:T(8,128)(2,1)} %get-tuple-element.7, pred[]{:T(512)S(6)} %eq.3), kind=kLoop, calls=%fused_computation.1 | loop fusion | flops 2621440 | bytes 4194305 | tf_op jit(solution)/shard_map/add | solution.py:396
